TPU v7x, 32 devices: a whole 2x2x4 slice. The times are simulated.
32 devices in a mesh: col: 4 (over z), row: 8 (over y, x, core).
Axes of the slice: x: 2, y: 2, z: 4, core: 2. Of those that a mesh axis runs over, the one named last changes fastest.
Arguments:
- features: bfloat16 [65536, 384], P(('row', 'col'))
- w_hidden: bfloat16 [384, 512], replicated
- w_output: bfloat16 [512, 100], replicated
- adj_cols: int32 [32, 65536], P('col', 'row')
- adj_vals: bfloat16 [32, 65536], P('col', 'row')
- adj_mask: int32 [32, 65536], P('col', 'row')
- labels: int32 [65536], P(('row', 'col'))
- train_mask: int32 [65536], P(('row', 'col'))
Outputs:
- output 1: float32 [], replicated
- output 2: float32 [384, 512], replicated
- output 3: float32 [512, 100], replicated
All inputs are finite; a program needn't handle non-finite values.
Results may differ from a plain program's by a relative error of at most 0.00102.
Values are sent between devices in bfloat16 or wider.
A program may use at most 1 GiB of HBM per device.

v0:
```python
import jax
import jax.numpy as jnp
from jax import lax
from jax.sharding import PartitionSpec as P

CONTRACT_ROWS = (((0,), (0,)), ((), ()))
CONTRACT_COLS = (((1,), (1,)), ((), ()))


def gather_apply(col_ids_all, weights, dense):
    def slot_step(running, slot):
        col_ids, slot_w = slot
        return running + slot_w[:, None] * jnp.take(dense, col_ids, axis=0), None
    zero_acc = jnp.zeros((col_ids_all.shape[1], dense.shape[1]), jnp.float32)
    summed, _ = lax.scan(slot_step, zero_acc, (col_ids_all, weights))
    return summed


def scatter_apply(col_ids_all, weights, dense, num_out):
    def slot_step(running, slot):
        col_ids, slot_w = slot
        return running + jax.ops.segment_sum(slot_w[:, None] * dense, col_ids, num_segments=num_out), None
    zero_acc = jnp.zeros((num_out, dense.shape[1]), jnp.float32)
    summed, _ = lax.scan(slot_step, zero_acc, (col_ids_all, weights))
    return summed


def solution(mesh):
    row_size = mesh.shape["row"]
    col_size = mesh.shape["col"]
    both_axes = ("col", "row")
    to_source = [(col_j * row_size + row_i, row_i * col_size + col_j) for row_i in range(row_size) for col_j in range(col_size)]
    to_dest = [(flat_idx, (flat_idx % col_size) * row_size + flat_idx // col_size) for flat_idx in range(row_size * col_size)]

    def device_step(feat_blk, w_hidden, w_output, cols_blk, vals_blk, mask_blk, labels_blk, train_blk):
        col_nodes = feat_blk.shape[0] * row_size
        weights = vals_blk.astype(jnp.float32) * mask_blk.astype(jnp.float32)
        feat_src = lax.ppermute(feat_blk, both_axes, to_source)
        proj_one = jnp.dot(feat_src, w_hidden, preferred_element_type=jnp.float32).astype(jnp.bfloat16)
        dense_one = lax.all_gather(proj_one, "row", axis=0, tiled=True)
        part_one = gather_apply(cols_blk, weights, dense_one)
        z_one = lax.psum_scatter(part_one, "col", scatter_dimension=0, tiled=True).astype(jnp.bfloat16)
        h_one = jnp.maximum(z_one, 0)
        proj_two = jnp.dot(h_one, w_output, preferred_element_type=jnp.float32).astype(jnp.bfloat16)
        proj_src = lax.ppermute(proj_two, both_axes, to_source)
        dense_two = lax.all_gather(proj_src, "row", axis=0, tiled=True)
        part_two = gather_apply(cols_blk, weights, dense_two)
        z_two = lax.psum_scatter(part_two, "col", scatter_dimension=0, tiled=True)
        mask_f = train_blk.astype(jnp.float32)
        train_count = jnp.maximum(lax.psum(jnp.sum(train_blk), both_axes), 1).astype(jnp.float32)
        log_norm = jax.nn.logsumexp(z_two, axis=1)
        onehot = (labels_blk[:, None] == jnp.arange(z_two.shape[1], dtype=jnp.int32)[None, :]).astype(jnp.float32)
        picked = jnp.sum(z_two * onehot, axis=1)
        loss_mean = lax.psum(jnp.sum(mask_f * (log_norm - picked)), both_axes) / train_count
        softmax_z = jnp.exp(z_two - log_norm[:, None])
        grad_two = ((mask_f / train_count)[:, None] * (softmax_z - onehot)).astype(jnp.bfloat16)
        grad_rows = lax.all_gather(grad_two, "col", axis=0, tiled=True)
        part_back = scatter_apply(cols_blk, weights, grad_rows, col_nodes)
        back_src = lax.psum_scatter(part_back, "row", scatter_dimension=0, tiled=True).astype(jnp.bfloat16)
        back_two = lax.ppermute(back_src, both_axes, to_dest)
        grad_w_output = lax.dot_general(h_one, back_two, CONTRACT_ROWS, preferred_element_type=jnp.float32)
        dh_one = lax.dot_general(back_two, w_output, CONTRACT_COLS, preferred_element_type=jnp.float32)
        dz_one = jnp.where(z_one > 0, dh_one, 0.0).astype(jnp.bfloat16)
        dz_rows = lax.all_gather(dz_one, "col", axis=0, tiled=True)
        part_dz = scatter_apply(cols_blk, weights, dz_rows, col_nodes)
        back_one = lax.psum_scatter(part_dz, "row", scatter_dimension=0, tiled=True).astype(jnp.bfloat16)
        grad_w_hidden = lax.dot_general(feat_src, back_one, CONTRACT_ROWS, preferred_element_type=jnp.float32)
        grad_w_hidden = lax.psum(grad_w_hidden, both_axes)
        grad_w_output = lax.psum(grad_w_output, both_axes)
        return loss_mean, grad_w_hidden, grad_w_output

    node_spec = P(("row", "col"), None)
    label_spec = P(("row", "col"))
    adj_spec = P("col", "row")
    return jax.shard_map(device_step, mesh=mesh, in_specs=(node_spec, P(), P(), adj_spec, adj_spec, adj_spec, label_spec, label_spec), out_specs=(P(), P(), P()), check_vma=False)
```

profile of v0, /device:TPU:0, one launch (start us, length us, event | category | flops | bytes accessed | tf_op | source)
XLA Modules:
  0.0 3056.2 jit_solution(14775249978602660280)
XLA Ops:
  13.4 195.6 %all-gather.5.cloned.1.call-done = bf16[16384,512]{1,0:T(8,128)(2,1)} async-done(((bf16[2048,512]{1,0:T(8,128)(2,1)}), bf16[16384,512]{1,0:T(8,128)(2,1)}) %all-gather.5.cloned.1.call-update) | async-done | bytes 16777232 | tf_op jit(solution)/shard_map/all_gather | solution.py:40
  209.0 467.1 %while.44 = (s32[]{:T(128)}, f32[8192,512]{1,0:T(8,128)}, f32[8,8192]{1,0:T(8,128)S(1)}, s32[8,8192]{1,0:T(8,128)S(1)}, bf16[16384,512]{1,0:T(8,128)(2,1)}, /*index=5*/s32[]{:T(128)}, s32[]{:T(128)}) while((s32[]{:T(128)}, f32[8192,512]{1,0:T(8,128)}, f32[8,8192]{1,0:T(8,128)S(1)}, s32[8,8192]{1,0:T(8,128)S(1)}, ...), condition=%wide.region_1.2_spmd.clone, body=%wide.region_0.1_spmd.clone.sunk | while | flops 21053444 | bytes 59064420 | solution.py:15
  676.2 279.3 %reduce-scatter.5.cloned.1.call-done = f32[2048,512]{1,0:T(8,128)} async-done(((f32[8192,512]{1,0:T(8,128)}), f32[2048,512]{1,0:T(8,128)}) %reduce-scatter.5.cloned.1.call-update) | async-done | bytes 4194320 | tf_op jit(solution)/shard_map/reduce_scatter | solution.py:42
  960.1 63.9 %all-gather.7.cloned.1.call-done = bf16[16384,100]{0,1:T(8,128)(2,1)} async-done(((bf16[2048,100]{0,1:T(8,128)(2,1)}), bf16[16384,100]{0,1:T(8,128)(2,1)}) %all-gather.7.cloned.1.call-update) | async-done | bytes 3276816 | tf_op jit(solution)/shard_map/all_gather | solution.py:46
  1030.1 274.6 %while.45 = (s32[]{:T(128)}, f32[8192,100]{1,0:T(8,128)}, f32[8,8192]{1,0:T(8,128)S(1)}, s32[8,8192]{1,0:T(8,128)S(1)}, bf16[16384,100]{1,0:T(8,128)(2,1)}, /*index=5*/s32[]{:T(128)}, s32[]{:T(128)}) while((s32[]{:T(128)}, f32[8192,100]{1,0:T(8,128)}, f32[8,8192]{1,0:T(8,128)S(1)}, s32[8,8192]{1,0:T(8,128)S(1)}, ...), condition=%wide.region_4.5_spmd.clone, body=%wide.region_3.4_spmd.clone.sunk | while | flops 4177923 | bytes 11812967 | solution.py:15
  1440.4 402.2 %while.42 = (s32[]{:T(128)}, f32[16384,100]{1,0:T(8,128)}, s32[8,8192]{1,0:T(8,128)S(1)}, f32[8,8192]{1,0:T(8,128)S(1)}, bf16[8192,100]{1,0:T(8,128)(2,1)S(1)}, /*index=5*/s32[]{:T(128)}) while((s32[]{:T(128)}, f32[16384,100]{1,0:T(8,128)}, s32[8,8192]{1,0:T(8,128)S(1)}, f32[8,8192]{1,0:T(8,128)S(1)}, bf16[8192,100]{1,0:T(8,128)(2,1)S(1)}, ...), condition=%wide.region_15.16_spmd, body=%wide.region_13.15_spmd.sunk | while | flops 2457602 | bytes 8814677 | solution.py:24
  1440.5 50.2 %scatter_custom_fusion.9 = f32[16384,100]{1,0:T(8,128)} fusion(f32[16384,100]{1,0:T(8,128)} %get-tuple-element.399, s32[8192]{0:T(1024)S(1)} %bitcast.55, bf16[8192,100]{1,0:T(8,128)(2,1)S(1)} %get-tuple-element.408, f32[8192]{0:T(1024)S(1)} %bitcast.48), kind=kCustom, calls=%fused_computation.4.clone.1 | custom fusion | flops 2457600 | bytes 8683520 | tf_op jit(solution)/shard_map/while/body/eval_jaxpr/scatter-add | solution.py:22
  1490.8 50.2 %scatter_custom_fusion.9 = f32[16384,100]{1,0:T(8,128)} fusion(f32[16384,100]{1,0:T(8,128)} %get-tuple-element.399, s32[8192]{0:T(1024)S(1)} %bitcast.55, bf16[8192,100]{1,0:T(8,128)(2,1)S(1)} %get-tuple-element.408, f32[8192]{0:T(1024)S(1)} %bitcast.48), kind=kCustom, calls=%fused_computation.4.clone.1 | custom fusion | flops 2457600 | bytes 8683520 | tf_op jit(solution)/shard_map/while/body/eval_jaxpr/scatter-add | solution.py:22
  1541.1 50.2 %scatter_custom_fusion.9 = f32[16384,100]{1,0:T(8,128)} fusion(f32[16384,100]{1,0:T(8,128)} %get-tuple-element.399, s32[8192]{0:T(1024)S(1)} %bitcast.55, bf16[8192,100]{1,0:T(8,128)(2,1)S(1)} %get-tuple-element.408, f32[8192]{0:T(1024)S(1)} %bitcast.48), kind=kCustom, calls=%fused_computation.4.clone.1 | custom fusion | flops 2457600 | bytes 8683520 | tf_op jit(solution)/shard_map/while/body/eval_jaxpr/scatter-add | solution.py:22
  1591.3 50.2 %scatter_custom_fusion.9 = f32[16384,100]{1,0:T(8,128)} fusion(f32[16384,100]{1,0:T(8,128)} %get-tuple-element.399, s32[8192]{0:T(1024)S(1)} %bitcast.55, bf16[8192,100]{1,0:T(8,128)(2,1)S(1)} %get-tuple-element.408, f32[8192]{0:T(1024)S(1)} %bitcast.48), kind=kCustom, calls=%fused_computation.4.clone.1 | custom fusion | flops 2457600 | bytes 8683520 | tf_op jit(solution)/shard_map/while/body/eval_jaxpr/scatter-add | solution.py:22
  1641.6 50.2 %scatter_custom_fusion.9 = f32[16384,100]{1,0:T(8,128)} fusion(f32[16384,100]{1,0:T(8,128)} %get-tuple-element.399, s32[8192]{0:T(1024)S(1)} %bitcast.55, bf16[8192,100]{1,0:T(8,128)(2,1)S(1)} %get-tuple-element.408, f32[8192]{0:T(1024)S(1)} %bitcast.48), kind=kCustom, calls=%fused_computation.4.clone.1 | custom fusion | flops 2457600 | bytes 8683520 | tf_op jit(solution)/shard_map/while/body/eval_jaxpr/scatter-add | solution.py:22
  1842.7 69.7 %reduce-scatter.9.cloned.1.call-done = f32[2048,100]{1,0:T(8,128)} async-done(((f32[16384,100]{1,0:T(8,128)}), f32[2048,100]{1,0:T(8,128)}) %reduce-scatter.9.cloned.1.call-update) | async-done | bytes 819216 | tf_op jit(solution)/shard_map/reduce_scatter | solution.py:59
  1918.7 176.6 %all-gather.11.cloned.1.call-done = bf16[8192,512]{1,0:T(8,128)(2,1)} async-done(((bf16[2048,512]{1,0:T(8,128)(2,1)}), bf16[8192,512]{1,0:T(8,128)(2,1)}) %all-gather.11.cloned.1.call-update) | async-done | bytes 8388624 | tf_op jit(solution)/shard_map/all_gather | solution.py:64
  2106.6 598.5 %while.43 = (s32[]{:T(128)}, f32[16384,512]{1,0:T(8,128)}, s32[8,8192]{1,0:T(8,128)S(1)}, f32[8,8192]{1,0:T(8,128)S(1)}, bf16[8192,512]{1,0:T(8,128)(2,1)}, /*index=5*/s32[]{:T(128)}) while((s32[]{:T(128)}, f32[16384,512]{1,0:T(8,128)}, s32[8,8192]{1,0:T(8,128)S(1)}, f32[8,8192]{1,0:T(8,128)S(1)}, bf16[8192,512]{1,0:T(8,128)(2,1)}, ...), condition=%wide.region_19.20_spmd, body=%wide.region_17.19_spmd.sunk | while | flops 12582914 | bytes 42106964 | solution.py:24
  2106.7 74.7 %scatter_custom_fusion.11 = f32[16384,512]{1,0:T(8,128)} fusion(f32[16384,512]{1,0:T(8,128)} %get-tuple-element.417, s32[8192]{0:T(1024)S(1)} %bitcast.56, bf16[8192,512]{1,0:T(8,128)(2,1)} %get-tuple-element.426, f32[8192]{0:T(1024)S(1)} %bitcast.54), kind=kCustom, calls=%fused_computation.10.clone.1 | custom fusion | flops 12582912 | bytes 41975808 | tf_op jit(solution)/shard_map/while/body/eval_jaxpr/scatter-add | solution.py:22
  2181.5 74.7 %scatter_custom_fusion.11 = f32[16384,512]{1,0:T(8,128)} fusion(f32[16384,512]{1,0:T(8,128)} %get-tuple-element.417, s32[8192]{0:T(1024)S(1)} %bitcast.56, bf16[8192,512]{1,0:T(8,128)(2,1)} %get-tuple-element.426, f32[8192]{0:T(1024)S(1)} %bitcast.54), kind=kCustom, calls=%fused_computation.10.clone.1 | custom fusion | flops 12582912 | bytes 41975808 | tf_op jit(solution)/shard_map/while/body/eval_jaxpr/scatter-add | solution.py:22
  2256.3 74.7 %scatter_custom_fusion.11 = f32[16384,512]{1,0:T(8,128)} fusion(f32[16384,512]{1,0:T(8,128)} %get-tuple-element.417, s32[8192]{0:T(1024)S(1)} %bitcast.56, bf16[8192,512]{1,0:T(8,128)(2,1)} %get-tuple-element.426, f32[8192]{0:T(1024)S(1)} %bitcast.54), kind=kCustom, calls=%fused_computation.10.clone.1 | custom fusion | flops 12582912 | bytes 41975808 | tf_op jit(solution)/shard_map/while/body/eval_jaxpr/scatter-add | solution.py:22
  2331.1 74.7 %scatter_custom_fusion.11 = f32[16384,512]{1,0:T(8,128)} fusion(f32[16384,512]{1,0:T(8,128)} %get-tuple-element.417, s32[8192]{0:T(1024)S(1)} %bitcast.56, bf16[8192,512]{1,0:T(8,128)(2,1)} %get-tuple-element.426, f32[8192]{0:T(1024)S(1)} %bitcast.54), kind=kCustom, calls=%fused_computation.10.clone.1 | custom fusion | flops 12582912 | bytes 41975808 | tf_op jit(solution)/shard_map/while/body/eval_jaxpr/scatter-add | solution.py:22
  2405.9 74.7 %scatter_custom_fusion.11 = f32[16384,512]{1,0:T(8,128)} fusion(f32[16384,512]{1,0:T(8,128)} %get-tuple-element.417, s32[8192]{0:T(1024)S(1)} %bitcast.56, bf16[8192,512]{1,0:T(8,128)(2,1)} %get-tuple-element.426, f32[8192]{0:T(1024)S(1)} %bitcast.54), kind=kCustom, calls=%fused_computation.10.clone.1 | custom fusion | flops 12582912 | bytes 41975808 | tf_op jit(solution)/shard_map/while/body/eval_jaxpr/scatter-add | solution.py:22
  2480.7 74.7 %scatter_custom_fusion.11 = f32[16384,512]{1,0:T(8,128)} fusion(f32[16384,512]{1,0:T(8,128)} %get-tuple-element.417, s32[8192]{0:T(1024)S(1)} %bitcast.56, bf16[8192,512]{1,0:T(8,128)(2,1)} %get-tuple-element.426, f32[8192]{0:T(1024)S(1)} %bitcast.54), kind=kCustom, calls=%fused_computation.10.clone.1 | custom fusion | flops 12582912 | bytes 41975808 | tf_op jit(solution)/shard_map/while/body/eval_jaxpr/scatter-add | solution.py:22
  2555.5 74.7 %scatter_custom_fusion.11 = f32[16384,512]{1,0:T(8,128)} fusion(f32[16384,512]{1,0:T(8,128)} %get-tuple-element.417, s32[8192]{0:T(1024)S(1)} %bitcast.56, bf16[8192,512]{1,0:T(8,128)(2,1)} %get-tuple-element.426, f32[8192]{0:T(1024)S(1)} %bitcast.54), kind=kCustom, calls=%fused_computation.10.clone.1 | custom fusion | flops 12582912 | bytes 41975808 | tf_op jit(solution)/shard_map/while/body/eval_jaxpr/scatter-add | solution.py:22
  2630.3 74.7 %scatter_custom_fusion.11 = f32[16384,512]{1,0:T(8,128)} fusion(f32[16384,512]{1,0:T(8,128)} %get-tuple-element.417, s32[8192]{0:T(1024)S(1)} %bitcast.56, bf16[8192,512]{1,0:T(8,128)(2,1)} %get-tuple-element.426, f32[8192]{0:T(1024)S(1)} %bitcast.54), kind=kCustom, calls=%fused_computation.10.clone.1 | custom fusion | flops 12582912 | bytes 41975808 | tf_op jit(solution)/shard_map/while/body/eval_jaxpr/scatter-add | solution.py:22
  2708.6 199.6 %reduce-scatter.11.cloned.1.call-done = f32[2048,512]{1,0:T(8,128)} async-done(((f32[16384,512]{1,0:T(8,128)}), f32[2048,512]{1,0:T(8,128)}) %reduce-scatter.11.cloned.1.call-update) | async-done | bytes 4194320 | tf_op jit(solution)/shard_map/reduce_scatter | solution.py:66
  2953.0 91.7 %all-reduce.3.cloned.1.call-done = (f32[384,512]{0,1:T(8,128)}, f32[512,100]{0,1:T(8,128)}) async-done(((f32[384,512]{0,1:T(8,128)}, f32[512,100]{0,1:T(8,128)}), (f32[384,512]{0,1:T(8,128)}, f32[512,100]{0,1:T(8,128)})) %all-reduce.3.cloned.1.call-update) | async-done | bytes 991248 | tf_op jit(solution)/shard_map/psum | solution.py:68
  (203 shorter events, 1113.6 us)
Async XLA Ops:
  7.2 3.5 copy-start
  7.2 6.1 copy-start.8
  7.2 6.1 copy-start.9
  7.2 201.8 %copy-start.3 = (s32[8,8192]{1,0:T(8,128)S(1)}, s32[8,8192]{1,0:T(8,128)}, u32[]{:S(2)}) copy-start(s32[8,8192]{1,0:T(8,128)} %param.19) | copy-start | bytes 786436
  7.2 201.8 %all-gather.5.cloned.1.call-start = ((), (), s32[]{:S(2)}) async-start(), calls=%async_computation.4 | async-start | bytes 18874368 | tf_op jit(solution)/shard_map/all_gather | solution.py:40
  7.3 2.2 collective-permute-start
  9.5 1.2 copy-start.4
  13.2 942.3 %reduce-scatter.5.cloned.1.call-start = ((), (), s32[]{:S(2)}) async-start(), calls=%async_computation.5 | async-start | bytes 20971520 | tf_op jit(solution)/shard_map/reduce_scatter | solution.py:42
  676.2 279.4 %copy-start.7 = (bf16[512,100]{0,1:T(8,128)(2,1)S(1)}, bf16[512,100]{0,1:T(8,128)(2,1)}, u32[]{:S(2)}) copy-start(bf16[512,100]{0,1:T(8,128)(2,1)} %param.18) | copy-start | bytes 307204
  676.2 347.8 %all-gather.7.cloned.1.call-start = ((), (), s32[]{:S(2)}) async-start(), calls=%async_computation.6 | async-start | bytes 3833856 | tf_op jit(solution)/shard_map/all_gather | solution.py:46
  958.5 0.7 collective-permute-start.1
  959.2 0.8 copy-start.6
  960.0 422.9 %reduce-scatter.7.cloned.1.call-start = ((), (), s32[]{:S(2)}) async-start(), calls=%async_computation.7 | async-start | bytes 5242880 | tf_op jit(solution)/shard_map/reduce_scatter | solution.py:48
  1304.7 0.7 copy-start.11
  1304.7 79.7 %copy-start.10 = (s32[2048]{0:T(1024)S(1)}, s32[2048]{0:T(1024)}, u32[]{:S(2)}) copy-start(s32[2048]{0:T(1024)} %param.22) | copy-start | bytes 24580
  1304.7 132.2 %all-gather.9.cloned.1.call-start = ((), (), s32[]{:S(2)}) async-start(), calls=%async_computation.8 | async-start | bytes 2621440 | tf_op jit(solution)/shard_map/all_gather | solution.py:57
  1391.1 521.3 %reduce-scatter.9.cloned.1.call-start = ((), (), s32[]{:S(2)}) async-start(), calls=%async_computation.9 | async-start | bytes 9437184 | tf_op jit(solution)/shard_map/reduce_scatter | solution.py:59
  1436.9 3.5 copy-start.2
  1842.7 252.7 %all-gather.11.cloned.1.call-start = ((), (), s32[]{:S(2)}) async-start(), calls=%async_computation.10 | async-start | bytes 10485760 | tf_op jit(solution)/shard_map/all_gather | solution.py:64
  1913.7 0.7 collective-permute-start.2
  1918.7 989.6 %reduce-scatter.11.cloned.1.call-start = ((), (), s32[]{:S(2)}) async-start(), calls=%async_computation.11 | async-start | bytes 37748736 | tf_op jit(solution)/shard_map/reduce_scatter | solution.py:66
  2705.1 203.1 %copy-start.5 = (bf16[2048,384]{1,0:T(8,128)(2,1)S(1)}, bf16[2048,384]{1,0:T(8,128)(2,1)}, u32[]{:S(2)}) copy-start(bf16[2048,384]{1,0:T(8,128)(2,1)} %copy-done.4) | copy-start | bytes 4718596
  2705.1 339.5 %all-reduce.3.cloned.1.call-start = ((), (), s32[]{:S(2)}) async-start(), calls=%async_computation.12 | async-start | bytes 1998848 | tf_op jit(solution)/shard_map/psum | solution.py:68
  2705.2 343.4 %copy-start.1 = (bf16[384,512]{1,0:T(8,128)(2,1)S(1)}, bf16[384,512]{1,0:T(8,128)(2,1)}, u32[]{:S(2)}) copy-start(bf16[384,512]{1,0:T(8,128)(2,1)} %param.17) | copy-start | bytes 1179652
Sparse Core Ops, SparseCore 0:
  13.4 195.5 all-gather.4
  676.3 279.1 reduce-scatter.4
  960.1 63.8 all-gather.6
  1304.9 77.9 reduce-scatter.6
  1391.3 45.6 all-gather.8
  1842.8 69.5 reduce-scatter.8
  1918.8 176.5 all-gather.10
  2705.2 202.9 reduce-scatter.10
  2914.1 130.5 all-reduce.2
where the time goes:
time: 3060 us
  other arithmetic  1220 us (40%)
  waiting for transfers between devices  1160 us (38%)
  local copies, waits for them, and re-layouts  560 us (18%)
  blocking collectives  81 us (3%)
    scatter-add x16, other arithmetic, slot_step(): jax.ops.segment_sum(slot_w[:, None] * dense, col_ids, num_segments=num_out)  1000 us
    gather x16, local copies, waits for them, and re-layouts, slot_step(): return (running + slot_w[:, None] * jnp.take(dense, col_ids, axis=0), None)  531 us
    reduce_scatter x1, waiting for transfers between devices, device_step(): lax.psum_scatter(part_one, 'col', scatter_dimension=0, tiled=True)  279 us
    add x16, other arithmetic, slot_step(): return (running + slot_w[:, None] * jnp.take(dense, col_ids, axis=0), None)  208 us
    reduce_scatter x1, waiting for transfers between devices, device_step(): lax.psum_scatter(part_dz, 'row', scatter_dimension=0, tiled=True)  200 us
    all_gather x1, waiting for transfers between devices, device_step(): dense_one = lax.all_gather(proj_one, 'row', axis=0, tiled=True)  196 us
    all_gather x1, waiting for transfers between devices, device_step(): dz_rows = lax.all_gather(dz_one, 'col', axis=0, tiled=True)  177 us
    psum x1, waiting for transfers between devices, device_step(): grad_w_hidden = lax.psum(grad_w_hidden, both_axes)  91.7 us
  transfers between devices with their start and end apart: 12, of which 9 were waited for; matrix products, arithmetic and copies ran while one was open for 0% of the time, Pallas kernels for 0%

commit v1 on v0

v1 whole, which is shorter than its diff:
```python
import functools

import jax
import jax.numpy as jnp
from jax import lax
from jax.experimental import pallas as pl
from jax.experimental.pallas import tpu as pltpu
from jax.sharding import PartitionSpec as P

CONTRACT_ROWS = (((0,), (0,)), ((), ()))
CONTRACT_COLS = (((1,), (1,)), ((), ()))
LANES = 128
VMEM_LIMIT = 66 * 1000 * 1000
F32 = jnp.float32
BF16 = jnp.bfloat16


def gather_hidden_kernel(build_steps, tile, unroll, x_ref, w_ref, ids_ref, wts_ref, z_ref, table, total):
    phase, step = pl.program_id(0), pl.program_id(1)
    groups = w_ref.shape[1] // LANES
    in_rows = x_ref.shape[0]
    slots, rows = ids_ref.shape

    @pl.when(step < build_steps)
    def _():
        def build(t, carry):
            x = x_ref[pl.ds(pl.multiple_of(t * tile, tile), tile), :]
            base = (step * in_rows + t * tile) * groups
            y = jnp.dot(x, w_ref[...], preferred_element_type=F32).astype(BF16).astype(F32)
            for g in range(groups):
                table[pl.ds(base + g, tile, stride=groups), :] = y[:, g * LANES:(g + 1) * LANES]
            return carry
        lax.fori_loop(0, in_rows // tile, build, 0)

    @pl.when(step >= build_steps)
    def _():
        first = (step - build_steps) * rows

        def rows_of(t, carry):
            sums = []
            for u in range(unroll):
                r = t * unroll + u
                acc = None
                for s in range(slots):
                    row = table[pl.ds(pl.multiple_of(ids_ref[s, r], groups), groups), :]
                    term = wts_ref[s, r] * row
                    acc = term if acc is None else acc + term
                sums.append(acc)
            for u in range(unroll):
                at = pl.ds(pl.multiple_of((first + t * unroll + u) * groups, groups), groups)
                total[at, :] = jnp.where(phase > 0, total[at, :], 0.0) + sums[u]
            return carry
        lax.fori_loop(0, rows // unroll, rows_of, 0)

        @pl.when(phase == pl.num_programs(0) - 1)
        def _():
            def finish(t, carry):
                start = pl.multiple_of(first + t * tile, tile)
                for g in range(groups):
                    part = total[pl.ds(start * groups + g, tile, stride=groups), :]
                    z_ref[pl.ds(start, tile), g * LANES:(g + 1) * LANES] = part.astype(BF16)
                return carry
            lax.fori_loop(0, rows // tile, finish, 0)


def gather_hidden(x_all, w_hidden, ids, wts):
    phases, slots = 4, ids.shape[0] // 4
    nodes, feat = x_all.shape
    hid = w_hidden.shape[1]
    groups = hid // LANES
    rows = ids.shape[1]
    block_nodes = nodes // phases
    in_rows, row_block = 2048, 512
    build_steps, gather_steps = block_nodes // in_rows, rows // row_block
    edge_spec = pl.BlockSpec((slots, row_block), lambda p, s: (p, jnp.maximum(s - build_steps, 0)), memory_space=pltpu.SMEM)
    return pl.pallas_call(
        functools.partial(gather_hidden_kernel, build_steps, 256, 4),
        grid=(phases, build_steps + gather_steps),
        out_shape=jax.ShapeDtypeStruct((rows, hid), BF16),
        in_specs=[
            pl.BlockSpec((in_rows, feat), lambda p, s: (p * build_steps + jnp.minimum(s, build_steps - 1), 0)),
            pl.BlockSpec((feat, hid), lambda p, s: (0, 0)),
            edge_spec,
            edge_spec,
        ],
        out_specs=pl.BlockSpec((rows, hid), lambda p, s: (0, 0)),
        scratch_shapes=[pltpu.VMEM((block_nodes * groups, LANES), F32), pltpu.VMEM((rows * groups, LANES), F32)],
        compiler_params=pltpu.CompilerParams(vmem_limit_bytes=VMEM_LIMIT, dimension_semantics=("arbitrary", "arbitrary")),
        name="gather_hidden",
    )(x_all, w_hidden, ids, wts)


def gather_class_kernel(build_steps, tile, unroll, p_ref, ids_ref, wts_ref, z_ref, table):
    step = pl.program_id(0)
    in_rows = p_ref.shape[0]
    slots, rows = ids_ref.shape

    @pl.when(step < build_steps)
    def _():
        def build(t, carry):
            at = pl.multiple_of(t * tile, tile)
            table[pl.ds(pl.multiple_of(step * in_rows + at, tile), tile), :] = p_ref[pl.ds(at, tile), :].astype(F32)
            return carry
        lax.fori_loop(0, in_rows // tile, build, 0)

    @pl.when(step >= build_steps)
    def _():
        first = (step - build_steps) * rows

        def rows_of(t, carry):
            for u in range(unroll):
                r = t * unroll + u
                accs = [None, None]
                for s in range(slots):
                    term = wts_ref[s, r] * table[pl.ds(ids_ref[s, r], 1), :]
                    accs[s % 2] = term if accs[s % 2] is None else accs[s % 2] + term
                z_ref[pl.ds(first + r, 1), :] = accs[0] + accs[1]
            return carry
        lax.fori_loop(0, rows // unroll, rows_of, 0)


def gather_class(p_all, ids, wts):
    nodes, width = p_all.shape
    slots, rows = ids.shape
    in_rows, row_block = 8192, 256
    build_steps, gather_steps = nodes // in_rows, rows // row_block
    edge_spec = pl.BlockSpec((slots, row_block), lambda s: (0, jnp.maximum(s - build_steps, 0)), memory_space=pltpu.SMEM)
    return pl.pallas_call(
        functools.partial(gather_class_kernel, build_steps, 256, 2),
        grid=(build_steps + gather_steps,),
        out_shape=jax.ShapeDtypeStruct((rows, width), F32),
        in_specs=[pl.BlockSpec((in_rows, width), lambda s: (jnp.minimum(s, build_steps - 1), 0)), edge_spec, edge_spec],
        out_specs=pl.BlockSpec((rows, width), lambda s: (0, 0)),
        scratch_shapes=[pltpu.VMEM((nodes, width), F32)],
        compiler_params=pltpu.CompilerParams(vmem_limit_bytes=VMEM_LIMIT, dimension_semantics=("arbitrary",)),
        name="gather_class",
    )(p_all, ids, wts)


HALF = 128


def scatter_kernel(groups, pairs, same_ref, ids_ref, wts_ref, d_ref, out_ref, rows_f, acc, sem):
    step = pl.program_id(0)
    slots, rows = ids_ref.shape

    @pl.when(step == 0)
    def _():
        def clear(t, carry):
            acc[pl.ds(pl.multiple_of(t * 256, 256), 256), :] = jnp.zeros((256, LANES), F32)
            return carry
        lax.fori_loop(0, acc.shape[0] // 256, clear, 0)

    for g in range(groups):
        rows_f[pl.ds(g, rows, stride=groups), :] = d_ref[:, g * LANES:(g + 1) * LANES].astype(F32)

    def at_of(s, r):
        return pl.ds(pl.multiple_of(ids_ref[s, r], groups), groups)

    def source(r):
        return rows_f[pl.ds(pl.multiple_of(r * groups, groups), groups), :]

    for block in range(rows // (2 * HALF)):
        def batch(t, carry):
            same = same_ref[block, t * pairs]
            for k in range(1, pairs):
                same = same + same_ref[block, t * pairs + k]

            @pl.when(same == 0)
            def _():
                for k in range(pairs):
                    both = (block * 2 * HALF + t * pairs + k, block * 2 * HALF + HALF + t * pairs + k)
                    places, sums = [], []
                    for r in both:
                        d = source(r)
                        for s in range(slots):
                            at = at_of(s, r)
                            places.append(at)
                            sums.append(acc[at, :] + wts_ref[s, r] * d)
                    for at, value in zip(places, sums):
                        acc[at, :] = value

            @pl.when(same != 0)
            def _():
                for k in range(pairs):
                    for h in range(2):
                        r = block * 2 * HALF + h * HALF + t * pairs + k
                        d = source(r)

                        def one(s, c):
                            at = at_of(s, r)
                            acc[at, :] = acc[at, :] + wts_ref[s, r] * d
                            return c
                        lax.fori_loop(0, slots, one, 0)
            return carry
        lax.fori_loop(0, HALF // pairs, batch, 0)

    @pl.when(step == pl.num_programs(0) - 1)
    def _():
        copy = pltpu.make_async_copy(acc, out_ref, sem)
        copy.start()
        copy.wait()


def scatter_rows(same, ids, wts, dense, num_out):
    slots, rows = ids.shape
    groups = dense.shape[1] // LANES
    row_block = 1024
    blocks = row_block // (2 * HALF)
    edge_spec = pl.BlockSpec((slots, row_block), lambda s: (0, s), memory_space=pltpu.SMEM)
    return pl.pallas_call(
        functools.partial(scatter_kernel, groups, 2),
        grid=(rows // row_block,),
        out_shape=jax.ShapeDtypeStruct((num_out * groups, LANES), F32),
        in_specs=[
            pl.BlockSpec((None, blocks, HALF), lambda s: (s, 0, 0), memory_space=pltpu.SMEM),
            edge_spec,
            edge_spec,
            pl.BlockSpec((row_block, groups * LANES), lambda s: (s, 0)),
        ],
        out_specs=pl.BlockSpec(memory_space=pl.ANY),
        scratch_shapes=[
            pltpu.VMEM((row_block * groups, LANES), F32),
            pltpu.VMEM((num_out * groups, LANES), F32),
            pltpu.SemaphoreType.DMA,
        ],
        compiler_params=pltpu.CompilerParams(vmem_limit_bytes=VMEM_LIMIT, dimension_semantics=("arbitrary",)),
        name=f"scatter_rows_{groups}",
    )(same.reshape(rows // row_block, blocks, HALF), ids, wts, dense)


def shared_ids(ids):
    slots, rows = ids.shape
    blocks = ids.reshape(slots, rows // (2 * HALF), 2, HALF)
    each = [blocks[s, :, h] for s in range(slots) for h in range(2)]
    same = jnp.zeros(each[0].shape, jnp.bool_)
    for a in range(len(each)):
        for b in range(a):
            same = same | (each[a] == each[b])
    return same.astype(jnp.int32)


def solution(mesh):
    row_size = mesh.shape["row"]
    col_size = mesh.shape["col"]
    both_axes = ("col", "row")
    node_axes = ("row", "col")
    to_dest = [(flat_idx, (flat_idx % col_size) * row_size + flat_idx // col_size) for flat_idx in range(row_size * col_size)]

    def device_step(feat_blk, w_hidden, w_output, cols_blk, vals_blk, mask_blk, labels_blk, train_blk):
        blk_nodes = feat_blk.shape[0]
        col_nodes = blk_nodes * row_size
        slots = cols_blk.shape[0]
        hid, classes = w_output.shape
        groups = hid // LANES
        masked = jnp.where(mask_blk > 0, vals_blk, jnp.zeros_like(vals_blk))
        weights = masked.astype(F32)
        w_out = jnp.pad(w_output, ((0, 0), (0, LANES - classes)))
        lane = jnp.arange(LANES, dtype=jnp.int32)[None, :]

        x_all = lax.all_gather(feat_blk, node_axes, axis=0, tiled=True)
        own_ids = lax.all_to_all(cols_blk.reshape(slots, col_size, blk_nodes), "col", 1, 0).reshape(slots * col_size, blk_nodes)
        own_wts = lax.all_to_all(masked.reshape(slots, col_size, blk_nodes), "col", 1, 0).reshape(slots * col_size, blk_nodes).astype(F32)
        same = shared_ids(cols_blk)

        z_one = gather_hidden(x_all, w_hidden, own_ids * groups, own_wts)
        h_one = jnp.maximum(z_one, 0)
        proj_two = jnp.dot(h_one, w_out, preferred_element_type=F32).astype(BF16)
        count = jnp.sum(train_blk)
        extra = jnp.where(lane == classes, count // 64, jnp.where(lane == classes + 1, count % 64, 0)).astype(BF16)
        proj_two = jnp.where(lane < classes, proj_two, extra)
        p_all = lax.all_gather(proj_two, node_axes, axis=0, tiled=True)
        counts = p_all.reshape(row_size * col_size, blk_nodes, LANES)[:, 0, classes:classes + 2].astype(F32)
        train_count = jnp.maximum(jnp.sum(counts[:, 0] * 64.0 + counts[:, 1]), 1.0)

        starts = (jnp.arange(slots * col_size, dtype=jnp.int32) // slots) * col_nodes
        z_two = gather_class(p_all, own_ids + starts[:, None], own_wts)
        mask_f = train_blk.astype(F32)
        z_two = jnp.where(lane < classes, z_two, -jnp.inf)
        peak = jnp.max(z_two, axis=1, keepdims=True)
        exps = jnp.exp(z_two - peak)
        log_norm = jnp.log(jnp.sum(exps, axis=1, keepdims=True)) + peak
        onehot = labels_blk[:, None] == lane
        picked = jnp.sum(jnp.where(onehot, z_two, 0.0), axis=1)
        loss_part = jnp.sum(mask_f * (log_norm[:, 0] - picked)) / train_count
        softmax_z = jnp.exp(z_two - log_norm)
        grad_two = ((mask_f / train_count)[:, None] * (softmax_z - onehot.astype(F32))).astype(BF16)

        grad_rows = lax.all_gather(grad_two, "col", axis=0, tiled=True)
        part_back = scatter_rows(same, cols_blk, weights, grad_rows, col_nodes)
        back_src = lax.psum_scatter(part_back, "row", scatter_dimension=0, tiled=True).astype(BF16)
        back_two = lax.ppermute(back_src, both_axes, to_dest)
        grad_w_output = lax.dot_general(h_one, back_two, CONTRACT_ROWS, preferred_element_type=F32)
        dh_one = lax.dot_general(back_two, w_out, CONTRACT_COLS, preferred_element_type=F32)
        dz_one = jnp.where(z_one > 0, dh_one, 0.0).astype(BF16)
        dz_rows = lax.all_gather(dz_one, "col", axis=0, tiled=True)
        part_dz = scatter_rows(same, cols_blk * groups, weights, dz_rows, col_nodes)
        back_one = lax.psum_scatter(part_dz, "row", scatter_dimension=0, tiled=True).astype(BF16).reshape(blk_nodes, hid)
        src_blk = lax.axis_index("col") * row_size + lax.axis_index("row")
        feat_src = lax.dynamic_slice_in_dim(x_all, src_blk * blk_nodes, blk_nodes, axis=0)
        grad_w_hidden = lax.dot_general(feat_src, back_one, CONTRACT_ROWS, preferred_element_type=F32)
        tail = jnp.where((lane == classes) & (jnp.arange(hid)[:, None] == 0), loss_part, 0.0)
        grad_w_output = jnp.where(lane < classes, grad_w_output, tail)
        grad_w_hidden, grad_w_output = lax.psum((grad_w_hidden, grad_w_output), both_axes)
        return grad_w_output[0, classes], grad_w_hidden, grad_w_output[:, :classes]

    node_spec = P(("row", "col"), None)
    label_spec = P(("row", "col"))
    adj_spec = P("col", "row")
    return jax.shard_map(device_step, mesh=mesh, in_specs=(node_spec, P(), P(), adj_spec, adj_spec, adj_spec, label_spec, label_spec), out_specs=(P(), P(), P()), check_vma=False)
```

time: 3060 us -> 1810 us (0.59)
  other arithmetic: 1220 us -> 18.4 us
  Pallas kernels: 0 us -> 744 us
  local copies, waits for them, and re-layouts: 560 us -> 12.2 us
  waiting for transfers between devices: 1160 us -> 998 us
  blocking collectives: 81 us -> 0 us
    scatter-add x16 -> x0, other arithmetic: 1000 us -> none  [slot_step(): jax.ops.segment_sum(slot_w[:, None] * dense, col_ids, num_segments=num_out)]
    pallas_call x0 -> x4, Pallas kernels: none -> 744 us  [the longest x2 456 us: scatter_rows(): pl.pallas_call(functools.partial(scatter_kernel, groups, 2), grid=(rows /...]
    gather x16 -> x0, local copies, waits for them, and re-layouts: 531 us -> none  [slot_step(): return (running + slot_w[:, None] * jnp.take(dense, col_ids, axis=0), None)]
    reduce_scatter x2 -> x0, waiting for transfers between devices: 314 us -> none  [the longest x1 279 us: device_step(): lax.psum_scatter(part_one, 'col', scatter_dimension=0, tiled=True)]
    add x16 -> x1, other arithmetic: 208 us -> 0.82 us  [device_step(): z_two = gather_class(p_all, own_ids + starts[:, None], own_wts)]
    all_gather x2, waiting for transfers between devices: 260 us -> 365 us  [the longest x1 252 us: device_step(): x_all = lax.all_gather(feat_blk, node_axes, axis=0, tiled=True)]
    psum x2 -> x0, blocking collectives: 81 us -> none  [the longest x1 41.3 us: device_step(): lax.psum(jnp.sum(train_blk), both_axes)]
    psum x1, waiting for transfers between devices: 91.7 us -> 131 us  [device_step(): lax.psum((grad_w_hidden, grad_w_output), both_axes)]
  transfers between devices with their start and end apart: 12 -> 10, of which waited for: 9 -> 9; matrix products, arithmetic and copies ran while one was open for 0% -> 1% of each run, Pallas kernels for 0% -> 0%
where the time goes in v1:
time: 1810 us
  waiting for transfers between devices  998 us (55%)
  Pallas kernels  744 us (41%)
  other arithmetic  18.4 us (1%)
  between operations  18.3 us (1%)
    pallas_call x2, Pallas kernels, scatter_rows(): pl.pallas_call(functools.partial(scatter_kernel, groups, 2), grid=(rows /...  456 us
    all_gather x1, waiting for transfers between devices, device_step(): x_all = lax.all_gather(feat_blk, node_axes, axis=0, tiled=True)  252 us
    reduce_scatter x1, waiting for transfers between devices, device_step(): lax.psum_scatter(part_dz, 'row', scatter_dimension=0, tiled=True)  200 us
    pallas_call x1, Pallas kernels, gather_hidden(): pl.pallas_call(functools.partial(gather_hidden_kernel, build_steps, 256,...  193 us
    all_gather x1, waiting for transfers between devices, device_step(): dz_rows = lax.all_gather(dz_one, 'col', axis=0, tiled=True)  175 us
    psum x1, waiting for transfers between devices, device_step(): lax.psum((grad_w_hidden, grad_w_output), both_axes)  131 us
    all_gather x1, waiting for transfers between devices, device_step(): p_all = lax.all_gather(proj_two, node_axes, axis=0, tiled=True)  113 us
    pallas_call x1, Pallas kernels, gather_class(): pl.pallas_call(functools.partial(gather_class_kernel, build_steps, 256, 2...  95.4 us
  transfers between devices with their start and end apart: 10, of which 9 were waited for; matrix products, arithmetic and copies ran while one was open for 1% of the time, Pallas kernels for 0%

profile of v1, /device:TPU:0, one launch (start us, length us, event | category | flops | bytes accessed | tf_op | source)
XLA Modules:
  0.0 1812.3 jit_solution(7184584316674818183)
XLA Ops:
  9.7 6.4 all-to-all-start.1
  19.4 3.2 all-to-all-done.1
  22.6 3.4 all-to-all-start
  26.8 13.7 all-to-all-done
  41.3 252.1 %all-gather.5.cloned.1.call-done.x_ref = bf16[65536,384]{1,0:T(8,128)(2,1)} async-done(((bf16[2048,384]{1,0:T(8,128)(2,1)}), bf16[65536,384]{1,0:T(8,128)(2,1)}) %all-gather.5.cloned.1.call-update) | async-done | bytes 50331664 | tf_op jit(solution)/shard_map/all_gather | solution.py:261
  293.4 192.6 %gather_hidden.1 = bf16[2048,512]{1,0:T(8,128)(2,1)} custom-call(bf16[65536,384]{1,0:T(8,128)(2,1)} %all-gather.5.cloned.1.call-done.x_ref, bf16[384,512]{1,0:T(8,128)(2,1)} %w_ref.1, s32[32,2048]{1,0:T(8,128)} %get-tuple-element.18.ids_ref, f32[32,2048]{1,0:T(8,128)} %convert_bitcast_fusion.wts_ref), custom_call_target="tpu_custom_call" | custom-call | tf_op jit(solution)/shard_map/gather_hidden/pallas_call | solution.py:76
  485.9 3.1 fusion
  489.1 113.1 %all-gather.7.cloned.1.call-done.p_ref = bf16[65536,128]{1,0:T(8,128)(2,1)} async-done(((bf16[2048,128]{1,0:T(8,128)(2,1)}), bf16[65536,128]{1,0:T(8,128)(2,1)}) %all-gather.7.cloned.1.call-update) | async-done | bytes 16777232 | tf_op jit(solution)/shard_map/all_gather | solution.py:272
  602.2 95.4 %gather_class.1 = f32[2048,128]{1,0:T(8,128)} custom-call(bf16[65536,128]{1,0:T(8,128)(2,1)} %all-gather.7.cloned.1.call-done.p_ref, s32[32,2048]{1,0:T(8,128)} %get-tuple-element.17.ids_ref, f32[32,2048]{1,0:T(8,128)} %convert_bitcast_fusion.wts_ref), custom_call_target="tpu_custom_call" | custom-call | tf_op jit(solution)/shard_map/gather_class/pallas_call | solution.py:128
  700.8 2.3 select_reduce_fusion
  704.4 2.3 multiply_convert_fusion
  706.8 2.7 fusion.21
  711.1 39.4 %all-gather.9.cloned.1.call-done.d_ref = bf16[8192,128]{1,0:T(8,128)(2,1)} async-done(((bf16[2048,128]{1,0:T(8,128)(2,1)}), bf16[8192,128]{1,0:T(8,128)(2,1)}) %all-gather.9.cloned.1.call-update) | async-done | bytes 2097168 | tf_op jit(solution)/shard_map/all_gather | solution.py:289
  750.5 222.3 %scatter_rows_1.1 = f32[16384,128]{1,0:T(8,128)} custom-call(s32[8,4,128]{2,1,0:T(4,128)} %or_convert_fusion.same_ref, s32[8,8192]{1,0:T(8,128)} %ids_ref.1, f32[8,8192]{1,0:T(8,128)} %get-tuple-element.15.wts_ref, bf16[8192,128]{1,0:T(8,128)(2,1)} %all-gather.9.cloned.1.call-done.d_ref), custom_call_target="tpu_custom_call" | custom-call | tf_op jit(solution)/shard_map/scatter_rows_1/pallas_call | solution.py:211
  972.9 69.4 %reduce-scatter.3.cloned.1.call-done = f32[2048,128]{1,0:T(8,128)} async-done(((f32[16384,128]{1,0:T(8,128)}), f32[2048,128]{1,0:T(8,128)}) %reduce-scatter.3.cloned.1.call-update) | async-done | bytes 1048592 | tf_op jit(solution)/shard_map/reduce_scatter | solution.py:291
  1044.3 2.0 select_convert_fusion
  1048.1 175.0 %all-gather.11.cloned.1.call-done.d_ref = bf16[8192,512]{1,0:T(8,128)(2,1)} async-done(((bf16[2048,512]{1,0:T(8,128)(2,1)}), bf16[8192,512]{1,0:T(8,128)(2,1)}) %all-gather.11.cloned.1.call-update) | async-done | bytes 8388624 | tf_op jit(solution)/shard_map/all_gather | solution.py:296
  1223.1 234.1 %scatter_rows_4.1 = f32[65536,128]{1,0:T(8,128)} custom-call(s32[8,4,128]{2,1,0:T(4,128)} %or_convert_fusion.same_ref, s32[8,8192]{1,0:T(8,128)} %broadcast_multiply_fusion.ids_ref, f32[8,8192]{1,0:T(8,128)} %get-tuple-element.15.wts_ref, bf16[8192,512]{1,0:T(8,128)(2,1)} %all-gather.11.cloned.1.call-done.d_ref), custom_call_target="tpu_custom_call" | custom-call | tf_op jit(solution)/shard_map/scatter_rows_4/pallas_call | solution.py:211
  1460.2 200.5 %reduce-scatter.5.cloned.1.call-done = f32[8192,128]{1,0:T(8,128)} async-done(((f32[65536,128]{1,0:T(8,128)}), f32[8192,128]{1,0:T(8,128)}) %reduce-scatter.5.cloned.1.call-update) | async-done | bytes 4194320 | tf_op jit(solution)/shard_map/reduce_scatter | solution.py:298
  1660.7 2.4 convert_element_type.68
  1663.1 2.6 reshape.220
  1665.7 4.0 fusion.4
  1669.7 130.7 %all-reduce.4.cloned.1.call-done = (f32[512,128]{1,0:T(8,128)}, f32[384,512]{1,0:T(8,128)}) async-done(((f32[512,128]{1,0:T(8,128)}, f32[384,512]{1,0:T(8,128)}), (f32[512,128]{1,0:T(8,128)}, f32[384,512]{1,0:T(8,128)})) %all-reduce.4.cloned.1.call-update) | async-done | bytes 1048592 | tf_op jit(solution)/shard_map/psum | solution.py:304
  1803.4 2.1 copy.67
  (50 shorter events, 19.5 us)
Async XLA Ops:
  7.2 8.9 copy-start.4
  7.2 286.2 %all-gather.5.cloned.1.call-start = ((), (), s32[]{:S(2)}) async-start(), calls=%async_computation.4 | async-start | bytes 51904512 | tf_op jit(solution)/shard_map/all_gather | solution.py:261
  9.7 12.8 all-to-all-start.1
  22.6 17.9 all-to-all-start
  26.0 576.2 %all-gather.7.cloned.1.call-start = ((), (), s32[]{:S(2)}) async-start(), calls=%async_computation.5 | async-start | bytes 17301504 | tf_op jit(solution)/shard_map/all_gather | solution.py:272
  293.4 192.6 %copy-start.5 = (bf16[512,100]{0,1:T(8,128)(2,1)S(1)}, bf16[512,100]{0,1:T(8,128)(2,1)}, u32[]{:S(2)}) copy-start(bf16[512,100]{0,1:T(8,128)(2,1)} %param.10) | copy-start | bytes 307204
  489.1 261.5 %all-gather.9.cloned.1.call-start = ((), (), s32[]{:S(2)}) async-start(), calls=%async_computation.6 | async-start | bytes 2621440 | tf_op jit(solution)/shard_map/all_gather | solution.py:289
  602.2 98.7 %copy-start.3 = (s32[2048]{0:T(1024)S(1)}, s32[2048]{0:T(1024)}, u32[]{:S(2)}) copy-start(s32[2048]{0:T(1024)} %param.14) | copy-start | bytes 24580
  697.5 6.9 copy-start
  706.7 335.6 %reduce-scatter.3.cloned.1.call-start = ((), (), s32[]{:S(2)}) async-start(), calls=%async_computation.7 | async-start | bytes 9437184 | tf_op jit(solution)/shard_map/reduce_scatter | solution.py:291
  972.8 71.5 %copy-start.1 = (bf16[2048,512]{1,0:T(8,128)(2,1)S(1)}, bf16[2048,512]{1,0:T(8,128)(2,1)}, u32[]{:S(2)}) copy-start(bf16[2048,512]{1,0:T(8,128)(2,1)} %gather_hidden.1) | copy-start | bytes 6291460
  972.8 250.2 %all-gather.11.cloned.1.call-start = ((), (), s32[]{:S(2)}) async-start(), calls=%async_computation.8 | async-start | bytes 10485760 | tf_op jit(solution)/shard_map/all_gather | solution.py:296
  1043.6 0.7 collective-permute-start
  1046.4 614.3 %reduce-scatter.5.cloned.1.call-start = ((), (), s32[]{:S(2)}) async-start(), calls=%async_computation.9 | async-start | bytes 37748736 | tf_op jit(solution)/shard_map/reduce_scatter | solution.py:298
  1457.2 1.6 copy-start.2
  1457.2 343.2 %all-reduce.4.cloned.1.call-start = ((), (), s32[]{:S(2)}) async-start(), calls=%async_computation.10 | async-start | bytes 2097152 | tf_op jit(solution)/shard_map/psum | solution.py:304
Sparse Core Ops, SparseCore 0:
  10.9 282.4 all-gather.4
  489.2 112.9 all-gather.6
  706.9 43.6 all-gather.8
  973.0 69.3 reduce-scatter.2
  1046.5 176.5 all-gather.10
  1457.3 203.3 reduce-scatter.4
  1669.8 130.5 all-reduce.3
